TPU v7x, 32 devices: a whole 2x2x4 slice. The times are simulated.
32 devices in a mesh: layer: 4 (over y, core), slab: 8 (over z, x).
Axes of the slice: x: 2, y: 2, z: 4, core: 2. Of those that a mesh axis runs over, the one named last changes fastest.
Arguments:
- weights: bfloat16 [8192, 16384], P('slab', 'layer'), may hold values from -0.29882812 to 0.29882812
- whitening: bfloat16 [8192, 8192], P('slab'), may hold values from -1 to 10, as said below
- test_matrix: int32 [16384, 1024], P(('layer', 'slab')), may hold values from -4 to 4
Outputs:
- basis: float32 [8192, 1024], P('slab')
- coefficients: float32 [16384, 1024], P('layer', 'slab')
Inputs may be any that keep to these rules, and one draw needn't show every extreme that they name: whitening is lower triangular with diagonal entries between 1 and 10.
All inputs are finite; a program needn't handle non-finite values.
Results may differ from a plain program's by a relative error of at most 0.006.
Values may be sent and summed in bfloat16 or wider, within the bound.
A program may use at most 128 MiB of HBM per device.

v0:
```python
import math

import jax
import jax.numpy as jnp
from jax import lax
from jax.sharding import PartitionSpec as P

D = 8192


def on_device(weights, whitening, test_matrix):
    rank_width = test_matrix.shape[1]
    slice_width = rank_width // lax.axis_size("layer")
    test_values = test_matrix.astype(jnp.bfloat16)
    columns = weights
    sketch_terms = jnp.dot(
        columns,
        lax.all_gather(test_values, "slab", axis=0, tiled=True),
        preferred_element_type=jnp.float32,
    )
    sketch = lax.psum_scatter(sketch_terms, "layer", scatter_dimension=1, tiled=True).astype(
        jnp.bfloat16
    )
    columns = whitening
    whitened_part = jnp.dot(
        columns,
        lax.all_gather(sketch, "slab", axis=0, tiled=True),
        preferred_element_type=jnp.float32,
    )
    whitened = lax.all_gather(whitened_part, "layer", axis=1, tiled=True)
    local_gram = jnp.dot(
        whitened.T, whitened, precision=lax.Precision.HIGHEST, preferred_element_type=jnp.float32
    )
    gram_matrix = lax.psum(local_gram, "slab")
    factor = jnp.linalg.cholesky(gram_matrix)
    ortho = jax.scipy.linalg.solve_triangular(factor, whitened.T, lower=True).T
    basis_half = ortho.astype(jnp.bfloat16)
    basis = basis_half.astype(jnp.float32) * math.sqrt(D)
    own_slice = lax.dynamic_slice_in_dim(
        basis_half, lax.axis_index("layer") * slice_width, slice_width, 1
    )
    columns = whitening
    projected_part = lax.psum_scatter(
        lax.dot_general(
            columns, own_slice, (((0,), (0,)), ((), ())), preferred_element_type=jnp.float32
        ),
        "slab",
        scatter_dimension=0,
        tiled=True,
    ).astype(jnp.bfloat16)
    projected = lax.all_gather(projected_part, "layer", axis=1, tiled=True)
    columns = weights
    coefficients = lax.psum_scatter(
        lax.dot_general(
            columns, projected, (((0,), (0,)), ((), ())), preferred_element_type=jnp.float32
        ),
        "slab",
        scatter_dimension=1,
        tiled=True,
    )
    return (basis, coefficients)


def solution(mesh):
    placed = (P("slab", "layer"), P("slab", None), P(("layer", "slab"), None))
    return jax.shard_map(
        on_device,
        mesh=mesh,
        in_specs=placed,
        out_specs=(P("slab", None), P("layer", "slab")),
        check_vma=False,
    )
```

profile of v0, /device:TPU:0, one launch (start us, length us, event | category | flops | bytes accessed | tf_op | source)
XLA Modules:
  0.0 1321.0 jit_solution(4433787939744664165)
XLA Ops:
  10.1 127.8 %all-gather.5.cloned.1.call-done = bf16[4096,1024]{1,0:T(8,128)(2,1)} async-done(((bf16[512,1024]{1,0:T(8,128)(2,1)}), bf16[4096,1024]{1,0:T(8,128)(2,1)}) %all-gather.5.cloned.1.call-update) | async-done | bytes 8388624 | tf_op jit(solution)/shard_map/all_gather | solution.py:18
  137.9 14.9 %fusion.73 = f32[1024,1024]{1,0:T(8,128)} fusion(bf16[1024,4096]{1,0:T(8,128)(2,1)} %param.3, bf16[4096,1024]{1,0:T(8,128)(2,1)} %all-gather.5.cloned.1.call-done), kind=kOutput, calls=%fused_computation.164 | convolution fusion | flops 8589934592 | bytes 20971520 | tf_op jit(solution)/shard_map/dot_general | solution.py:16
  152.9 42.7 %reduce-scatter.4.cloned.1.call-done = f32[1024,256]{1,0:T(8,128)} async-done(((f32[1024,1024]{1,0:T(8,128)}), f32[1024,256]{1,0:T(8,128)}) %reduce-scatter.4.cloned.1.call-update) | async-done | bytes 1048592 | tf_op jit(solution)/shard_map/reduce_scatter | solution.py:21
  197.8 73.4 %all-gather.7.cloned.1.call-done = bf16[8192,256]{1,0:T(8,128)(2,1)} async-done(((bf16[1024,256]{1,0:T(8,128)(2,1)}), bf16[8192,256]{1,0:T(8,128)(2,1)}) %all-gather.7.cloned.1.call-update) | async-done | bytes 4194320 | tf_op jit(solution)/shard_map/all_gather | solution.py:27
  271.1 12.6 convolution_bitcast_fusion.2
  284.0 32.9 %all-gather.9.cloned.1.call-done = f32[1024,1024]{0,1:T(8,128)} async-done(((f32[1024,256]{0,1:T(8,128)}), f32[1024,1024]{0,1:T(8,128)}) %all-gather.9.cloned.1.call-update) | async-done | bytes 4194320 | tf_op jit(solution)/shard_map/all_gather | solution.py:30
  316.9 18.2 %fusion.74 = f32[1024,1024]{0,1:T(8,128)} fusion(f32[1024,1024]{0,1:T(8,128)} %all-gather.9.cloned.1.call-done), kind=kOutput, calls=%fused_computation.165 | convolution fusion | flops 12884901888 | bytes 8388608 | tf_op jit(solution)/shard_map/dot_general | solution.py:31
  335.2 156.5 %all-reduce.3.cloned.1.call-done = f32[1024,1024]{0,1:T(8,128)} async-done(((f32[1024,1024]{0,1:T(8,128)}), f32[1024,1024]{0,1:T(8,128)}) %all-reduce.3.cloned.1.call-update) | async-done | bytes 4194320 | tf_op jit(solution)/shard_map/psum | solution.py:34
  491.6 5.7 copy.6
  503.8 11.7 cholesky.223
  515.5 9.8 custom-call.63
  531.8 11.9 cholesky.244
  544.3 9.8 custom-call.64
  557.4 11.7 cholesky.468
  570.4 9.8 custom-call.65
  583.7 11.9 cholesky.487
  596.9 9.8 custom-call.66
  610.1 11.7 cholesky.506
  623.1 10.2 custom-call.67
  636.6 11.7 cholesky.526
  649.6 9.8 custom-call.68
  662.4 11.9 cholesky.546
  675.5 9.8 custom-call.69
  688.0 11.7 cholesky.564
  711.4 22.8 %while.1 = (s32[]{:T(128)}, f32[1024,1024]{1,0:T(8,128)}, s32[8,2]{0,1:T(2,128)S(1)}, f32[8,128,128]{2,1,0:T(8,128)S(1)}, s32[]{:T(128)}) while((s32[]{:T(128)}, f32[1024,1024]{1,0:T(8,128)}, s32[8,2]{0,1:T(2,128)S(1)}, f32[8,128,128]{2,1,0:T(8,128)S(1)}, s32[]{:T(128)}) %tuple.58), condition=%wide.while_cond, body=%wide.while_body.sunk | while | flops 2 | bytes 131181 | solution.py:36
  734.2 78.8 %custom-call.70 = f32[8,128,128]{1,2,0:T(8,128)S(1)} custom-call(f32[8,128,128]{2,1,0:T(8,128)S(1)} %get-tuple-element.9), custom_call_target="InvertDiagBlocksLowerTriangular" | custom-call | tf_op jit(solution)/shard_map/jit(_solve_triangular)/triangular_solve | solution.py:36
  837.6 6.7 convolution_bitcast_fusion
  844.3 147.0 %reduce-scatter.6.cloned.1.call-done = f32[1024,256]{0,1:T(8,128)} async-done(((f32[8192,256]{0,1:T(8,128)}), f32[1024,256]{0,1:T(8,128)}) %reduce-scatter.6.cloned.1.call-update) | async-done | bytes 1048592 | tf_op jit(solution)/shard_map/reduce_scatter | solution.py:43
  993.5 21.8 %all-gather.11.cloned.1.call-done = bf16[1024,1024]{0,1:T(8,128)(2,1)} async-done(((bf16[1024,256]{0,1:T(8,128)(2,1)}), bf16[1024,1024]{0,1:T(8,128)(2,1)}) %all-gather.11.cloned.1.call-update) | async-done | bytes 2097168 | tf_op jit(solution)/shard_map/all_gather | solution.py:51
  1015.2 16.0 %convolution_bitcast_fusion.1 = f32[4096,1024]{0,1:T(8,128)} fusion(bf16[1024,1024]{0,1:T(8,128)(2,1)} %all-gather.11.cloned.1.call-done, bf16[1024,4096]{1,0:T(8,128)(2,1)} %param.3), kind=kOutput, calls=%fused_computation.3 | convolution fusion | flops 8589934592 | bytes 27262976 | tf_op jit(solution)/shard_map/dot_general | solution.py:54
  1033.7 5.3 copy.7
  1039.1 271.7 %reduce-scatter.8.cloned.1.call-done = f32[4096,128]{0,1:T(8,128)} async-done(((f32[4096,1024]{0,1:T(8,128)}), f32[4096,128]{0,1:T(8,128)}) %reduce-scatter.8.cloned.1.call-update) | async-done | bytes 2097168 | tf_op jit(solution)/shard_map/reduce_scatter | solution.py:53
  (122 shorter events, 105.8 us)
Async XLA Ops:
  7.2 130.7 %all-gather.5.cloned.1.call-start = ((), (), s32[]{:S(2)}) async-start(), calls=%async_computation.3 | async-start | bytes 9437184 | tf_op jit(solution)/shard_map/all_gather | solution.py:18
  10.0 185.6 %reduce-scatter.4.cloned.1.call-start = ((), (), s32[]{:S(2)}) async-start(), calls=%async_computation.4 | async-start | bytes 5242880 | tf_op jit(solution)/shard_map/reduce_scatter | solution.py:21
  152.9 118.3 %all-gather.7.cloned.1.call-start = ((), (), s32[]{:S(2)}) async-start(), calls=%async_computation.5 | async-start | bytes 4718592 | tf_op jit(solution)/shard_map/all_gather | solution.py:27
  197.7 119.2 %all-gather.9.cloned.1.call-start = ((), (), s32[]{:S(2)}) async-start(), calls=%async_computation.6 | async-start | bytes 5242880 | tf_op jit(solution)/shard_map/all_gather | solution.py:30
  283.7 207.9 %all-reduce.3.cloned.1.call-start = ((), (), s32[]{:S(2)}) async-start(), calls=%async_computation.7 | async-start | bytes 8388608 | tf_op jit(solution)/shard_map/psum | solution.py:34
  335.1 656.2 %reduce-scatter.6.cloned.1.call-start = ((), (), s32[]{:S(2)}) async-start(), calls=%async_computation.8 | async-start | bytes 9437184 | tf_op jit(solution)/shard_map/reduce_scatter | solution.py:43
  501.8 2.0 copy-start
  813.1 4.3 copy-start.1
  822.3 15.2 %slice-start = ((s8[16777216]{0:T(1024)(128)(4,1)}), s8[4194304]{0:T(1024)(128)(4,1)S(1)}, s32[]{:S(2)}) async-start(s8[16777216]{0:T(1024)(128)(4,1)} %bitcast.119), calls=%async_computation.11 | async-start | bytes 8388608
  825.5 12.0 slice-start.1
  826.0 11.6 slice-start.2
  829.7 7.9 slice-start.3
  844.3 171.0 %all-gather.11.cloned.1.call-start = ((), (), s32[]{:S(2)}) async-start(), calls=%async_computation.9 | async-start | bytes 2621440 | tf_op jit(solution)/shard_map/all_gather | solution.py:51
  993.4 317.4 %reduce-scatter.8.cloned.1.call-start = ((), (), s32[]{:S(2)}) async-start(), calls=%async_computation.10 | async-start | bytes 18874368 | tf_op jit(solution)/shard_map/reduce_scatter | solution.py:53
Sparse Core Ops, SparseCore 0:
  10.7 127.1 all-gather.4
  153.0 42.5 reduce-scatter.3
  198.3 72.7 all-gather.6
  283.9 32.9 all-gather.8
  335.2 156.3 all-reduce.2
  844.4 146.8 reduce-scatter.5
  993.5 21.6 all-gather.10
  1031.3 279.4 reduce-scatter.7
where the time goes:
time: 1330 us; the launch traced here: 1320 us
  waiting for transfers between devices  874 us (66%)
  other arithmetic  270 us (20%)
  matrix products  115 us (9%)
  local copies, waits for them, and re-layouts  42.1 us (3%)
  between operations  19.9 us (1%)
    reduce_scatter x1, waiting for transfers between devices, on_device(): lax.psum_scatter(lax.dot_general(columns, projected, (((0,), (0,)), ((),...  272 us
    another operation x30, other arithmetic, on_device(): factor = jnp.linalg.cholesky(gram_matrix)  172 us
    psum x1, waiting for transfers between devices, on_device(): gram_matrix = lax.psum(local_gram, 'slab')  156 us
    reduce_scatter x1, waiting for transfers between devices, on_device(): lax.psum_scatter(lax.dot_general(columns, own_slice, (((0,), (0,)), ((),...  147 us
    all_gather x1, waiting for transfers between devices, on_device(): lax.all_gather(test_values, 'slab', axis=0, tiled=True)  128 us
    another operation x3, other arithmetic, on_device(): ortho = jax.scipy.linalg.solve_triangular(factor, whitened.T, lower=True).T  83.7 us
    all_gather x1, waiting for transfers between devices, on_device(): lax.all_gather(sketch, 'slab', axis=0, tiled=True)  73.4 us
    reduce_scatter x1, waiting for transfers between devices, on_device(): lax.psum_scatter(sketch_terms, 'layer', scatter_dimension=1, tiled=True)  42.7 us
  transfers between devices with their start and end apart: 8, of which 8 were waited for; matrix products, arithmetic and copies ran while one was open for 1% of the time, Pallas kernels for 0%

commit v1 on v0

v1 whole, which is shorter than its diff:
```python
import functools
import math

import jax
import jax.numpy as jnp
from jax import lax
from jax.experimental import pallas as pl
from jax.experimental.pallas import tpu as pltpu
from jax.sharding import PartitionSpec as P

BLOCK = 128
PANEL = 32
GROUP = 8
HIGHEST = lax.Precision.HIGHEST


def inverse_factor_kernel(size, panel, block_ref, inverse_ref, work):
    rows = lax.broadcasted_iota(jnp.int32, (size, size), 0)
    lanes = lax.broadcasted_iota(jnp.int32, (size, size), 1)
    work[:, :size] = block_ref[...]
    work[:, size:] = (rows == lanes).astype(jnp.float32)
    place = lax.broadcasted_iota(jnp.int32, (panel, size), 0)
    for start in range(0, size, panel):
        halves = [work[start : start + panel, :size], work[start : start + panel, size:]]
        for group in range(0, panel, GROUP):
            spread = [
                jnp.broadcast_to(
                    halves[0][:, start + group + k : start + group + k + 1], (panel, size)
                )
                for k in range(GROUP)
            ]
            for k in range(GROUP):
                step = group + k
                scale = lax.rsqrt(spread[k][step : step + 1, :])
                factor = spread[k] * scale
                for later in range(k + 1, GROUP):
                    pivot = spread[later][step : step + 1, :] * scale
                    spread[later] = spread[later] - factor * pivot
                for i in range(2):
                    pivot_row = halves[i][step : step + 1, :] * scale
                    cleared = halves[i] - factor * pivot_row
                    halves[i] = jnp.where(
                        place == step, pivot_row, jnp.where(place > step, cleared, halves[i])
                    )
        inverse_ref[start : start + panel, :] = halves[1]
        if start + panel < size:
            for i in range(2):
                update = lax.dot_general(
                    halves[0],
                    halves[i],
                    (((0,), (0,)), ((), ())),
                    precision=HIGHEST,
                    preferred_element_type=jnp.float32,
                )
                half = slice(i * size, (i + 1) * size)
                work[start + panel :, half] = (
                    work[start + panel :, half] - update[start + panel :, :]
                )


def inverse_factor(stacked, size):
    corner = pl.BlockSpec((size, size), lambda i: (0, 0))
    return pl.pallas_call(
        functools.partial(inverse_factor_kernel, size, PANEL),
        grid=(1,),
        out_shape=jax.ShapeDtypeStruct((size, size), jnp.float32),
        in_specs=[corner],
        out_specs=corner,
        scratch_shapes=[pltpu.VMEM((size, 2 * size), jnp.float32)],
        name="inverse_factor",
    )(stacked)


def times_transposed(left, right):
    return lax.dot_general(
        left,
        right,
        (((1,), (1,)), ((), ())),
        precision=HIGHEST,
        preferred_element_type=jnp.float32,
    )


def orthogonal(gram_matrix, whitened):
    rank = gram_matrix.shape[0]
    block = min(BLOCK, rank)
    stacked = jnp.concatenate([gram_matrix, whitened], axis=0)
    solved = []
    for start in range(0, rank, block):
        rest = rank - start - block
        inverse = inverse_factor(stacked, block)
        panel = times_transposed(stacked[block:, :block], inverse)
        solved.append(panel[rest:])
        if rest > 0:
            stacked = stacked[block:, block:] - times_transposed(panel, panel[:rest])
    return jnp.concatenate(solved, axis=1)


def on_device(weights, whitening, test_matrix):
    rank_width = test_matrix.shape[1]
    slice_width = rank_width // lax.axis_size("layer")
    test_values = test_matrix.astype(jnp.bfloat16)
    sketch_terms = jnp.dot(
        weights,
        lax.all_gather(test_values, "slab", axis=0, tiled=True),
        preferred_element_type=jnp.float32,
    )
    sketch = lax.psum_scatter(sketch_terms, "layer", scatter_dimension=1, tiled=True).astype(
        jnp.bfloat16
    )
    whitened_part = jnp.dot(
        whitening,
        lax.all_gather(sketch, "slab", axis=0, tiled=True),
        preferred_element_type=jnp.float32,
    )
    whitened = lax.all_gather(whitened_part, "layer", axis=1, tiled=True)
    local_gram = lax.dot_general(
        whitened_part,
        whitened,
        (((0,), (0,)), ((), ())),
        precision=HIGHEST,
        preferred_element_type=jnp.float32,
    )
    gram_matrix = lax.all_gather(
        lax.psum(local_gram, "slab"), "layer", axis=0, tiled=True
    )
    ortho = orthogonal(gram_matrix, whitened)
    basis_half = ortho.astype(jnp.bfloat16)
    basis = basis_half.astype(jnp.float32) * math.sqrt(whitening.shape[1])
    own_slice = lax.dynamic_slice_in_dim(
        basis_half, lax.axis_index("layer") * slice_width, slice_width, 1
    )
    projected_part = lax.psum_scatter(
        lax.dot_general(
            whitening, own_slice, (((0,), (0,)), ((), ())), preferred_element_type=jnp.float32
        ).astype(jnp.bfloat16),
        "slab",
        scatter_dimension=0,
        tiled=True,
    )
    projected = lax.all_gather(projected_part, "layer", axis=1, tiled=True)
    coefficients = lax.psum_scatter(
        lax.dot_general(
            weights, projected, (((0,), (0,)), ((), ())), preferred_element_type=jnp.float32
        ).astype(jnp.bfloat16),
        "slab",
        scatter_dimension=1,
        tiled=True,
    ).astype(jnp.float32)
    return (basis, coefficients)


def solution(mesh):
    placed = (P("slab", "layer"), P("slab", None), P(("layer", "slab"), None))
    return jax.shard_map(
        on_device,
        mesh=mesh,
        in_specs=placed,
        out_specs=(P("slab", None), P("layer", "slab")),
        check_vma=False,
    )
```

time: 1330 us -> 857 us (0.64)
  other arithmetic: 270 us -> 7.46 us
  waiting for transfers between devices: 874 us -> 641 us
  Pallas kernels: 0 us -> 40.4 us
    another operation x33 -> x0, other arithmetic: 256 us -> none  [the longest x30 172 us: on_device(): factor = jnp.linalg.cholesky(gram_matrix)]
    reduce_scatter x2, waiting for transfers between devices: 419 us -> 227 us  [the longest x1 138 us: on_device(): lax.psum_scatter(lax.dot_general(weights, projected, (((0,), (0,)), ((),...]
    psum x1, waiting for transfers between devices: 156 us -> 78.4 us  [on_device(): lax.psum(local_gram, 'slab')]
    another operation x29 -> x0, matrix products: 46.3 us -> none  [the longest x15 23.4 us: on_device(): ortho = jax.scipy.linalg.solve_triangular(factor, whitened.T, lower=True).T]
    dot_general x5 -> x20, matrix products: 68.3 us -> 114 us  [the longest x15 55.7 us: times_transposed(): lax.dot_general(left, right, (((1,), (1,)), ((), ())), precision=HIGHEST,...]
    pallas_call x0 -> x8, Pallas kernels: none -> 40.4 us  [inverse_factor(): pl.pallas_call(functools.partial(inverse_factor_kernel, size, PANEL), gri...]
    all_gather x0 -> x1, waiting for transfers between devices: none -> 35 us  [on_device(): lax.all_gather(lax.psum(local_gram, 'slab'), 'layer', axis=0, tiled=True)]
    another operation x34 -> x0, local copies, waits for them, and re-layouts: 25.3 us -> none
  transfers between devices with their start and end apart: 8 -> 9, of which waited for: 8 -> 9; matrix products, arithmetic and copies ran while one was open for 1% -> 1% of each run, Pallas kernels for 0% -> 0%
where the time goes in v1:
time: 857 us; the launch traced here: 849 us
  waiting for transfers between devices  641 us (75%)
  matrix products  114 us (13%)
  Pallas kernels  40.4 us (5%)
  local copies, waits for them, and re-layouts  31 us (4%)
  between operations  14.4 us (2%)
    reduce_scatter x1, waiting for transfers between devices, on_device(): lax.psum_scatter(lax.dot_general(weights, projected, (((0,), (0,)), ((),...  138 us
    all_gather x1, waiting for transfers between devices, on_device(): lax.all_gather(test_values, 'slab', axis=0, tiled=True)  128 us
    reduce_scatter x1, waiting for transfers between devices, on_device(): lax.psum_scatter(lax.dot_general(whitening, own_slice, (((0,), (0,)), (()...  88.8 us
    psum x1, waiting for transfers between devices, on_device(): lax.psum(local_gram, 'slab')  78.4 us
    all_gather x1, waiting for transfers between devices, on_device(): lax.all_gather(sketch, 'slab', axis=0, tiled=True)  73.4 us
    dot_general x15, matrix products, times_transposed(): lax.dot_general(left, right, (((1,), (1,)), ((), ())), precision=HIGHEST,...  55.7 us
    reduce_scatter x1, waiting for transfers between devices, on_device(): lax.psum_scatter(sketch_terms, 'layer', scatter_dimension=1, tiled=True)  42.7 us
    pallas_call x8, Pallas kernels, inverse_factor(): pl.pallas_call(functools.partial(inverse_factor_kernel, size, PANEL), gri...  40.4 us
  transfers between devices with their start and end apart: 9, of which 9 were waited for; matrix products, arithmetic and copies ran while one was open for 1% of the time, Pallas kernels for 0%

profile of v1, /device:TPU:0, one launch (start us, length us, event | category | flops | bytes accessed | tf_op | source)
XLA Modules:
  0.0 849.1 jit_solution(10726921238125649764)
XLA Ops:
  7.2 2.8 convert_element_type.25
  10.1 127.8 %all-gather.6.cloned.1.call-done = bf16[4096,1024]{1,0:T(8,128)(2,1)} async-done(((bf16[512,1024]{1,0:T(8,128)(2,1)}), bf16[4096,1024]{1,0:T(8,128)(2,1)}) %all-gather.6.cloned.1.call-update) | async-done | bytes 8388624 | tf_op jit(solution)/shard_map/all_gather | solution.py:105
  137.9 15.0 %fusion.33 = f32[1024,1024]{1,0:T(8,128)} fusion(bf16[1024,4096]{1,0:T(8,128)(2,1)} %param.3, bf16[4096,1024]{1,0:T(8,128)(2,1)} %all-gather.6.cloned.1.call-done), kind=kOutput, calls=%fused_computation.53 | convolution fusion | flops 8589934592 | bytes 20971520 | tf_op jit(solution)/shard_map/dot_general | solution.py:103
  152.9 42.7 %reduce-scatter.4.cloned.1.call-done = f32[1024,256]{1,0:T(8,128)} async-done(((f32[1024,1024]{1,0:T(8,128)}), f32[1024,256]{1,0:T(8,128)}) %reduce-scatter.4.cloned.1.call-update) | async-done | bytes 1048592 | tf_op jit(solution)/shard_map/reduce_scatter | solution.py:108
  197.8 73.4 %all-gather.8.cloned.1.call-done = bf16[8192,256]{1,0:T(8,128)(2,1)} async-done(((bf16[1024,256]{1,0:T(8,128)(2,1)}), bf16[8192,256]{1,0:T(8,128)(2,1)}) %all-gather.8.cloned.1.call-update) | async-done | bytes 4194320 | tf_op jit(solution)/shard_map/all_gather | solution.py:113
  271.1 9.4 %fusion.34 = f32[256,1024]{1,0:T(8,128)S(1)} fusion(bf16[8192,256]{1,0:T(8,128)(2,1)} %all-gather.8.cloned.1.call-done, bf16[1024,8192]{1,0:T(8,128)(2,1)} %param.4), kind=kOutput, calls=%fused_computation.54 | convolution fusion | flops 4294967296 | bytes 22020096 | tf_op jit(solution)/shard_map/dot_general | solution.py:111
  281.9 33.1 %all-gather.10.cloned.1.call-done = f32[1024,1024]{1,0:T(8,128)} async-done(((f32[1024,256]{1,0:T(8,128)}), f32[1024,1024]{1,0:T(8,128)}) %all-gather.10.cloned.1.call-update) | async-done | bytes 4194320 | tf_op jit(solution)/shard_map/all_gather | solution.py:116
  315.0 6.8 fusion.35
  321.9 78.4 %all-reduce.2.cloned.1.call-done = f32[256,1024]{1,0:T(8,128)} async-done(((f32[256,1024]{1,0:T(8,128)}), f32[256,1024]{1,0:T(8,128)}) %all-reduce.2.cloned.1.call-update) | async-done | bytes 1048592 | tf_op jit(solution)/shard_map/psum | solution.py:125
  400.8 35.0 %all-gather.12.cloned.1.call-done = f32[1024,1024]{1,0:T(8,128)} async-done(((f32[256,1024]{1,0:T(8,128)}), f32[1024,1024]{1,0:T(8,128)}) %all-gather.12.cloned.1.call-update) | async-done | bytes 4194320 | tf_op jit(solution)/shard_map/all_gather | solution.py:124
  435.8 4.9 constant_dynamic-update-slice_fusion.1
  442.9 5.0 inverse_factor.8
  450.2 9.5 %slice_subtract_fusion.block_ref = f32[1920,896]{1,0:T(8,128)} fusion(f32[2048,1024]{1,0:T(8,128)} %constant_dynamic-update-slice_fusion.block_ref, f32[1920,128]{0,1:T(8,128)S(1)} %fusion.2), kind=kOutput, calls=%fused_computation.3 | convolution fusion | flops 2644131840 | bytes 15204352 | tf_op jit(solution)/shard_map/dot_general | solution.py:75
  460.4 5.0 inverse_factor.9
  468.5 8.2 slice_subtract_fusion.1.block_ref
  476.7 5.0 inverse_factor.10
  484.8 7.3 slice_subtract_fusion.2.block_ref
  492.0 5.0 inverse_factor.11
  499.9 5.6 convolution_subtract_fusion.block_ref
  505.6 5.1 inverse_factor.12
  513.5 3.3 convolution_subtract_fusion.1.block_ref
  516.8 5.2 inverse_factor.13
  526.1 5.0 inverse_factor.14
  532.9 3.3 convolution_subtract_fusion.3.block_ref
  536.1 5.0 inverse_factor.15
  552.1 12.5 %fusion = bf16[8192,256]{0,1:T(8,128)(2,1)} fusion(bf16[1024,8192]{1,0:T(8,128)(2,1)} %param.4, bf16[1024,1024]{0,1:T(8,128)(2,1)} %fusion.1, s32[]{:T(128)S(6)} %select_n.3), kind=kOutput, calls=%fused_computation.1 | convolution fusion | flops 4297064448 | bytes 21495812 | tf_op jit(solution)/shard_map/dot_general | solution.py:134
  564.6 88.8 %reduce-scatter.6.cloned.1.call-done = bf16[1024,256]{0,1:T(8,128)(2,1)} async-done(((bf16[8192,256]{0,1:T(8,128)(2,1)}), bf16[1024,256]{0,1:T(8,128)(2,1)}) %reduce-scatter.6.cloned.1.call-update) | async-done | bytes 524304 | tf_op jit(solution)/shard_map/reduce_scatter | solution.py:133
  653.5 23.7 %all-gather.14.cloned.1.call-done = bf16[1024,1024]{0,1:T(8,128)(2,1)} async-done(((bf16[1024,256]{0,1:T(8,128)(2,1)}), bf16[1024,1024]{0,1:T(8,128)(2,1)}) %all-gather.14.cloned.1.call-update) | async-done | bytes 2097168 | tf_op jit(solution)/shard_map/all_gather | solution.py:141
  677.2 14.7 %convert_bitcast_fusion = bf16[4096,1024]{0,1:T(8,128)(2,1)} fusion(bf16[1024,1024]{0,1:T(8,128)(2,1)} %all-gather.14.cloned.1.call-done, bf16[1024,4096]{1,0:T(8,128)(2,1)} %param.3), kind=kOutput, calls=%fused_computation.2 | convolution fusion | flops 8594128896 | bytes 18874368 | tf_op jit(solution)/shard_map/dot_general | solution.py:143
  693.5 2.6 convert_multiply_fusion
  696.1 5.4 copy.6
  701.5 138.0 %reduce-scatter.8.cloned.1.call-done = bf16[4096,128]{0,1:T(8,128)(2,1)} async-done(((bf16[4096,1024]{0,1:T(8,128)(2,1)}), bf16[4096,128]{0,1:T(8,128)(2,1)}) %reduce-scatter.8.cloned.1.call-update) | async-done | bytes 1048592 | tf_op jit(solution)/shard_map/reduce_scatter | solution.py:142
  (54 shorter events, 42.3 us)
Async XLA Ops:
  7.2 130.7 %all-gather.6.cloned.1.call-start = ((), (), s32[]{:S(2)}) async-start(), calls=%async_computation.3 | async-start | bytes 9437184 | tf_op jit(solution)/shard_map/all_gather | solution.py:105
  10.0 185.6 %reduce-scatter.4.cloned.1.call-start = ((), (), s32[]{:S(2)}) async-start(), calls=%async_computation.4 | async-start | bytes 5242880 | tf_op jit(solution)/shard_map/reduce_scatter | solution.py:108
  152.9 118.2 %all-gather.8.cloned.1.call-start = ((), (), s32[]{:S(2)}) async-start(), calls=%async_computation.5 | async-start | bytes 4718592 | tf_op jit(solution)/shard_map/all_gather | solution.py:113
  197.7 117.3 %all-gather.10.cloned.1.call-start = ((), (), s32[]{:S(2)}) async-start(), calls=%async_computation.6 | async-start | bytes 5242880 | tf_op jit(solution)/shard_map/all_gather | solution.py:116
  281.8 118.4 %all-reduce.2.cloned.1.call-start = ((), (), s32[]{:S(2)}) async-start(), calls=%async_computation.7 | async-start | bytes 2097152 | tf_op jit(solution)/shard_map/psum | solution.py:125
  321.8 113.9 %all-gather.12.cloned.1.call-start = ((), (), s32[]{:S(2)}) async-start(), calls=%async_computation.8 | async-start | bytes 5242880 | tf_op jit(solution)/shard_map/all_gather | solution.py:124
  400.3 253.1 %reduce-scatter.6.cloned.1.call-start = ((), (), s32[]{:S(2)}) async-start(), calls=%async_computation.9 | async-start | bytes 4718592 | tf_op jit(solution)/shard_map/reduce_scatter | solution.py:133
  435.8 4.9 copy-start.2
  467.6 0.9 copy-start.3
  483.8 0.9 copy-start.4
  499.0 0.9 copy-start.5
  505.6 8.0 copy-start
  512.7 0.9 copy-start.6
  516.8 7.0 copy-start.1
  564.6 112.6 %all-gather.14.cloned.1.call-start = ((), (), s32[]{:S(2)}) async-start(), calls=%async_computation.10 | async-start | bytes 2621440 | tf_op jit(solution)/shard_map/all_gather | solution.py:141
  653.4 186.2 %reduce-scatter.8.cloned.1.call-start = ((), (), s32[]{:S(2)}) async-start(), calls=%async_computation.11 | async-start | bytes 9437184 | tf_op jit(solution)/shard_map/reduce_scatter | solution.py:142
  692.0 1.6 copy-start.7
Sparse Core Ops, SparseCore 0:
  10.7 127.1 all-gather.5
  153.0 42.5 reduce-scatter.3
  198.3 72.7 all-gather.7
  282.0 32.9 all-gather.9
  322.0 78.2 all-reduce.1
  401.7 34.0 all-gather.11
  564.7 88.6 reduce-scatter.5
  655.0 22.1 all-gather.13
  692.1 147.4 reduce-scatter.7
